TPU v7x, 32 devices: a whole 2x2x4 slice. The times are simulated.
32 devices in a mesh: img: 4 (over y, core), proj: 8 (over z, x).
Axes of the slice: x: 2, y: 2, z: 4, core: 2. Of those that a mesh axis runs over, the one named last changes fastest.
Arguments:
- images: bfloat16 [512, 4096], P('img'), may hold values from -48 to 48
- projections: bfloat16 [2560, 4096], P('proj'), may hold values from -6 to 6
- noise_weight: float32 [4096], replicated, may hold values from 0.02 to 0.08
- defocus: float32 [512], P('img'), may hold values from 2 to 8
- orient_count: int32 [512], P('img'), may hold values from 160 to 2560, as said below
- term_limit: int32 [512], P('img'), may hold values from 2048 to 4096
- block_plan: int32 [16], replicated, may hold values from 0 to 15, each once
Outputs:
- reconstruction: bfloat16 [2560, 4096], P('proj', 'img')
- evidence_next: float32 [512], P('img')
Inputs may be any that keep to these rules, and one draw needn't show every extreme that they name: Orientations 0 to orient_count[i] - 1 are the significant ones of image i; some image has all 2560.
All inputs are finite; a program needn't handle non-finite values.
Results may differ from a plain program's by a relative error of at most 0.018.
Values may be sent and summed in bfloat16 or wider, within the bound.
A program may use at most 64 MiB of HBM per device.

v0:
```python
import math
import jax
import jax.numpy as jnp
from jax import lax
from jax.sharding import PartitionSpec as P

F = 4096
BLOCK = 32


def contrast_table(defocus, width):
    frequency = (jnp.arange(width, dtype=jnp.float32) + 1.0) / width
    return jnp.sin(2.0 * math.pi * defocus[:, None] * frequency[None, :] + 0.1)


def image_terms(pixels, noise_weight, defocus, limits):
    width = pixels.shape[1]
    contrast = contrast_table(defocus, width)
    keep_mask = (jnp.arange(width, dtype=jnp.int32)[None, :] < limits[:, None]).astype(jnp.float32)
    values = pixels.astype(jnp.float32)
    weighted = (keep_mask * noise_weight[None, :] * contrast * values).astype(jnp.bfloat16)
    weighted_sq = (keep_mask * noise_weight[None, :] * contrast * contrast).astype(jnp.bfloat16)
    back_images = (keep_mask * contrast * values).astype(jnp.bfloat16)
    return (weighted, weighted_sq, back_images)


def slice_weight_sums(every_post, focus_all, limit_all, start, slice_width, img_count, img_rows):
    term_ids = jnp.arange(slice_width, dtype=jnp.int32) + start
    term_float = term_ids.astype(jnp.float32)
    frequency = (term_float + 1.0) / F
    contrast = jnp.sin(2.0 * math.pi * focus_all[:, None] * frequency[None, :] + 0.1)
    keep_mask = (term_float[None, :] < limit_all[:, None]).astype(jnp.float32)
    rebuilt = (keep_mask * contrast * contrast).astype(jnp.bfloat16)
    rebuilt = rebuilt.reshape(img_count, img_rows, slice_width)
    partial_value = jnp.einsum(
        "jbi,bif->bjf", every_post, rebuilt, preferred_element_type=jnp.float32
    )
    partial_value = lax.optimization_barrier(partial_value.astype(jnp.bfloat16)).astype(jnp.float32)
    return jnp.sum(partial_value, axis=0)


def shards(images, projections, noise_weight, defocus, orient_count, term_limit, block_plan):
    proj_rows = projections.shape[0]
    img_rows = images.shape[0]
    weighted, weighted_sq, back_images = image_terms(images, noise_weight, defocus, term_limit)
    proj_sq = (projections.astype(jnp.float32) * projections.astype(jnp.float32)).astype(
        jnp.bfloat16
    )
    contract = (((1,), (1,)), ((), ()))
    scores = lax.dot_general(projections, weighted, contract, preferred_element_type=jnp.float32)
    scores = scores - 0.5 * lax.dot_general(
        proj_sq, weighted_sq, contract, preferred_element_type=jnp.float32
    )
    orient_ids = lax.axis_index("proj") * proj_rows + jnp.arange(proj_rows, dtype=jnp.int32)
    significant = orient_ids[:, None] < orient_count[None, :]
    local_peak = jnp.max(jnp.where(significant, scores, -1e30), axis=0)
    row_peak = lax.pmax(local_peak, "proj")
    safe = jnp.where(significant, scores, row_peak[None, :])
    local_mass = jnp.sum(jnp.where(significant, jnp.exp(safe - row_peak[None, :]), 0.0), axis=0)
    row_mass = lax.psum(local_mass, "proj")
    log_evidence = row_peak + jnp.log(row_mass)
    posterior = jnp.where(significant, jnp.exp(scores - log_evidence[None, :]), 0.0).astype(
        jnp.bfloat16
    )
    img_count = lax.axis_size("img")
    slice_width = F // img_count
    slice_start = lax.axis_index("img") * slice_width
    limit_float = term_limit.astype(jnp.float32)
    moved_images = lax.all_to_all(back_images, "img", split_axis=1, concat_axis=0, tiled=True)
    every_post = lax.all_gather(posterior, "img", axis=1, tiled=True)
    focus_all, limit_all = (
        lax.all_gather(defocus, "img", axis=0, tiled=True),
        lax.all_gather(limit_float, "img", axis=0, tiled=True),
    )
    every_post = every_post.reshape(proj_rows, img_count, img_rows)
    moved_images = moved_images.reshape(img_count, img_rows, slice_width)
    part_images = jnp.einsum(
        "jbi,bif->bjf", every_post, moved_images, preferred_element_type=jnp.float32
    )
    part_images = lax.optimization_barrier(part_images.astype(jnp.bfloat16)).astype(jnp.float32)
    sum_images = jnp.sum(part_images, axis=0)
    sum_weights = slice_weight_sums(
        every_post, focus_all, limit_all, slice_start, slice_width, img_count, img_rows
    )
    reconstruction = (sum_images / (sum_weights + 1.0)).astype(jnp.bfloat16)
    every_evidence = lax.all_gather(log_evidence, "img", axis=0, tiled=True)
    blocks = every_evidence.reshape(-1, BLOCK)
    local_blocks = img_rows // BLOCK
    slot_ids = lax.axis_index("img") * local_blocks + jnp.arange(local_blocks, dtype=jnp.int32)
    selector = (block_plan[None, :] == slot_ids[:, None]).astype(jnp.float32)
    own_blocks = jnp.dot(selector, blocks, precision=lax.Precision.HIGHEST)
    return (reconstruction, own_blocks.reshape(img_rows))


def solution(mesh):
    placed = (P("img", None), P("proj", None), P(), P("img"), P("img"), P("img"), P())
    return jax.shard_map(
        shards, mesh=mesh, in_specs=placed, out_specs=(P("proj", "img"), P("img")), check_vma=False
    )
```

profile of v0, /device:TPU:0, one launch (start us, length us, event | category | flops | bytes accessed | tf_op | source)
XLA Modules:
  0.0 115.0 jit_solution(12315028204032979167)
XLA Ops:
  0.6 0.0 copy-start.3
  0.7 0.7 broadcast_multiply_fusion.1
  1.3 1.6 %copy.15 = bf16[128,4096]{0,1:T(8,128)(2,1)S(1)} copy(bf16[128,4096]{1,0:T(8,128)(2,1)} %param.7) | data formatting | bytes 2097152 | tf_op args[0]
  2.9 0.0 copy-done.3
  2.9 8.5 %fusion.2 = bf16[128,4096]{0,1:T(8,128)(2,1)S(1)} fusion(bf16[128,4096]{0,1:T(8,128)(2,1)S(1)} %copy.15, f32[4096]{0:T(1024)S(1)} %add_multiply_fusion, f32[128]{0:T(128)S(1)} %broadcast_multiply_fusion.1, s32[128]{0:T(128)S(1)} %copy-done.3), kind=kLoop, calls=%fused_computation.8 | loop fusion | flops 3670016 | bytes 2114560 | tf_op jit(solution)/shard_map/convert_element_type | solution.py:23
  11.4 0.0 copy-start.5
  11.4 1.3 %copy.16 = bf16[128,4,1024]{2,0,1:T(8,128)(2,1)} copy(bf16[128,4,1024]{0,2,1:T(8,128)(2,1)S(1)} %bitcast.26) | data formatting | bytes 2097152 | tf_op jit(solution)/shard_map/all_to_all | solution.py:69
  12.7 4.3 %all-to-all-start = ((bf16[128,4,1024]{2,0,1:T(8,128)(2,1)}), bf16[128,4,1024]{2,0,1:T(8,128)(2,1)S(1)}, u32[]{:S(2)}, u32[]{:S(2)}) async-start(bf16[128,4,1024]{2,0,1:T(8,128)(2,1)} %copy.16), calls=%async_computation | async-start | bytes 2097152 | tf_op jit(solution)/shard_map/all_to_all | solution.py:69
  17.0 0.0 copy-done.5
  17.0 0.0 copy-start.1
  17.0 0.0 copy-start.4
  17.1 12.5 %convolution_bitcast_fusion = f32[320,128]{1,0:T(8,128)S(1)} fusion(bf16[320,4096]{1,0:T(8,128)(2,1)} %param.8, bf16[128,4096]{0,1:T(8,128)(2,1)S(1)} %copy.15, f32[4096]{0:T(1024)S(1)} %add_multiply_fusion, f32[128]{0:T(128)S(1)} %broadcast_multiply_fusion.1, f32[4096]{0:T(1024)S(1)} %copy-done.5, s32[128]{0:T(128)S(1)} %copy-done.3), kind=kOutput, calls=%fused_computation.19 | convolution fusion | flops 339738624 | bytes 3867648 | tf_op jit(solution)/shard_map/dot_general | solution.py:50
  29.5 0.0 copy-done.1
  29.5 0.0 copy-done.4
  29.6 0.0 copy-start.6
  29.6 0.0 copy-start.2
  29.6 8.2 %fusion.32 = (f32[128]{0:T(128)S(1)}, f32[320,128]{1,0:T(8,128)S(1)}) fusion(s32[128]{0:T(128)S(1)} %copy-done.1, s32[320]{0:T(512)S(1)} %iota_add_fusion, f32[320,128]{1,0:T(8,128)S(1)} %convolution_bitcast_fusion, f32[4096]{0:T(1024)S(1)} %add_multiply_fusion, f32[128]{0:T(128)S(1)} %broadcast_multiply_fusion.1, f32[4096]{0:T(1024)S(1)} %copy-done.5, ...), kind=kOutput, calls=%fused_computation.47 | convolution fusion | flops 343351168 | bytes 2985216 | tf_op jit(solution)/shard_map/dot_general | solution.py:51
  37.7 22.6 %pmax.7 = f32[128]{0:T(128)S(1)} all-reduce(f32[128]{0:T(128)S(1)} %get-tuple-element.2), channel_id=1, replica_groups=mesh['img'=4,'proj'=8] {'proj'}, use_global_device_ids=true, to_apply=%region_1.2 | all-reduce | flops 128 | bytes 1024 | tf_op jit(solution)/shard_map/pmax | solution.py:57
  60.3 0.1 fusion.35
  60.5 17.1 %psum.7 = f32[128]{0:T(128)S(1)} all-reduce(f32[128]{0:T(128)S(1)} %fusion.35), channel_id=1, replica_groups=mesh['img'=4,'proj'=8] {'proj'}, use_global_device_ids=true, to_apply=%region_3.4 | all-reduce | flops 128 | bytes 1024 | tf_op jit(solution)/shard_map/psum | solution.py:60
  77.6 0.1 fusion.36
  77.7 5.1 %all-gather.2 = f32[4,1,128]{2,1,0:T(1,128)S(1)} all-gather(f32[1,1,128]{2,1,0:T(1,128)S(1)} %bitcast.27), channel_id=1, replica_groups=mesh['img'=4,'proj'=8] {'img'}, dimensions={0}, use_global_device_ids=true | all-gather | bytes 2560 | tf_op jit(solution)/shard_map/all_gather | solution.py:86
  82.8 0.5 broadcast.84
  83.3 0.7 reduce.3
  84.0 0.1 reshape.73
  84.0 0.0 copy-done.6
  84.0 0.2 fusion.37
  84.2 0.6 reshape.74
  84.8 5.3 %all-gather = f32[4,1,128]{2,1,0:T(1,128)S(1)} all-gather(f32[1,1,128]{2,1,0:T(1,128)S(1)} %convert_bitcast_fusion), channel_id=1, replica_groups=mesh['img'=4,'proj'=8] {'img'}, dimensions={0}, use_global_device_ids=true | all-gather | bytes 2560 | tf_op jit(solution)/shard_map/all_gather | solution.py:73
  90.1 0.0 copy-done.2
  90.1 5.0 %all-gather.1 = f32[4,1,128]{2,1,0:T(1,128)S(1)} all-gather(f32[1,1,128]{2,1,0:T(1,128)S(1)} %bitcast.30), channel_id=1, replica_groups=mesh['img'=4,'proj'=8] {'img'}, dimensions={0}, use_global_device_ids=true | all-gather | bytes 2560 | tf_op jit(solution)/shard_map/all_gather | solution.py:72
  95.2 6.3 %all_gather.12 = bf16[320,512]{1,0:T(8,128)(2,1)S(1)} all-gather(bf16[320,128]{1,0:T(8,128)(2,1)S(1)} %fusion.36), channel_id=1, replica_groups=mesh['img'=4,'proj'=8] {'img'}, dimensions={1}, use_global_device_ids=true | all-gather | bytes 409600 | tf_op jit(solution)/shard_map/all_gather | solution.py:70
  101.5 9.4 %convolution_convert_fusion = bf16[4,320,1024]{2,1,0:T(8,128)(2,1)} fusion(f32[1024]{0:T(1024)S(1)} %add_multiply_fusion.1, f32[4,128]{1,0:T(4,128)S(1)} %bitcast.29, f32[4,128]{1,0:T(4,128)S(1)} %bitcast.28, f32[1024]{0:T(1024)S(1)} %add_convert_fusion, bf16[320,512]{1,0:T(8,128)(2,1)S(1)} %all_gather.12), kind=kOutput, calls=%fused_computation.14 | convolution fusion | flops 340000768 | bytes 2961408 | tf_op jit(solution)/shard_map/jbi,bif->bjf/dot_general | solution.py:35
  110.9 0.0 all-to-all-done
  110.9 0.0 copy-start
  110.9 0.8 convolution_convert_fusion.1
  111.8 0.9 copy-done
  112.7 1.2 %convert_reduce_fusion = (f32[320,1024]{1,0:T(8,128)S(1)}, f32[320,1024]{1,0:T(8,128)S(1)}) fusion(bf16[4,320,1024]{2,1,0:T(8,128)(2,1)S(1)} %copy-done, bf16[4,320,1024]{2,1,0:T(8,128)(2,1)S(1)} %convolution_convert_fusion.1), kind=kLoop, calls=%fused_computation | loop fusion | flops 4587520 | bytes 7864320 | tf_op jit(solution)/shard_map/reduce_sum | solution.py:39
  113.9 1.1 divide_convert_fusion
  (8 shorter events, 0.0 us)
Async XLA Ops:
  0.6 2.3 %copy-start.3 = (s32[128]{0:T(128)S(1)}, s32[128]{0:T(128)}, u32[]{:S(2)}) copy-start(s32[128]{0:T(128)} %param.12) | copy-start | bytes 1540
  11.4 5.6 %copy-start.5 = (f32[4096]{0:T(1024)S(1)}, f32[4096]{0:T(1024)}, u32[]{:S(2)}) copy-start(f32[4096]{0:T(1024)} %param.9) | copy-start | bytes 49156
  12.7 98.2 %all-to-all-start = ((bf16[128,4,1024]{2,0,1:T(8,128)(2,1)}), bf16[128,4,1024]{2,0,1:T(8,128)(2,1)S(1)}, u32[]{:S(2)}, u32[]{:S(2)}) async-start(bf16[128,4,1024]{2,0,1:T(8,128)(2,1)} %copy.16), calls=%async_computation | async-start | bytes 2097152 | tf_op jit(solution)/shard_map/all_to_all | solution.py:69
  17.0 12.5 %copy-start.1 = (s32[128]{0:T(128)S(1)}, s32[128]{0:T(128)}, u32[]{:S(2)}) copy-start(s32[128]{0:T(128)} %param.11) | copy-start | bytes 1540
  17.0 12.5 %copy-start.4 = (bf16[320,4096]{1,0:T(8,128)(2,1)S(1)}, bf16[320,4096]{1,0:T(8,128)(2,1)}, u32[]{:S(2)}) copy-start(bf16[320,4096]{1,0:T(8,128)(2,1)} %param.8) | copy-start | bytes 7864324
  29.6 54.5 %copy-start.6 = (s32[16]{0:T(128)S(1)}, s32[16]{0:T(128)}, u32[]{:S(2)}) copy-start(s32[16]{0:T(128)} %param.13) | copy-start | bytes 196
  29.6 60.6 %copy-start.2 = (f32[128]{0:T(128)S(1)}, f32[128]{0:T(128)}, u32[]{:S(2)}) copy-start(f32[128]{0:T(128)} %param.10) | copy-start | bytes 1540
  110.9 1.7 %copy-start = (bf16[4,320,1024]{2,1,0:T(8,128)(2,1)S(1)}, bf16[4,320,1024]{2,1,0:T(8,128)(2,1)}, u32[]{:S(2)}) copy-start(bf16[4,320,1024]{2,1,0:T(8,128)(2,1)} %convolution_convert_fusion) | copy-start | bytes 7864324
where the time goes:
time: 115 us
  blocking collectives  61.5 us (53%)
  matrix products  31 us (27%)
  other arithmetic  12.4 us (11%)
  local copies, waits for them, and re-layouts  5.05 us (4%)
  starting transfers between devices  4.26 us (4%)
    pmax x1, blocking collectives, shards(): row_peak = lax.pmax(local_peak, 'proj')  22.6 us
    psum x1, blocking collectives, shards(): row_mass = lax.psum(local_mass, 'proj')  17.1 us
    dot_general x1, matrix products, shards(): lax.dot_general(projections, weighted, contract, preferred_element_type=j...  12.5 us
    dot_general x1, matrix products, slice_weight_sums(): jnp.einsum('jbi,bif->bjf', every_post, rebuilt, preferred_element_type=jn...  9.38 us
    convert_element_type x1, other arithmetic, image_terms(): back_images = (keep_mask * contrast * values).astype(jnp.bfloat16)  8.45 us
    dot_general x1, matrix products, shards(): lax.dot_general(proj_sq, weighted_sq, contract, preferred_element_type=jn...  8.17 us
    all_gather x1, blocking collectives, shards(): every_post = lax.all_gather(posterior, 'img', axis=1, tiled=True)  6.34 us
    all_gather x1, blocking collectives, shards(): lax.all_gather(limit_float, 'img', axis=0, tiled=True)  5.29 us
  transfers between devices with their start and end apart: 1, of which 0 were waited for; matrix products, arithmetic and copies ran while one was open for 28% of the time, Pallas kernels for 0%

commit v1 on v0

--- a/solution.py
+++ b/solution.py
@@ -6,6 +6,24 @@
 
 F = 4096
 BLOCK = 32
+
+
+def ring_gather(shard, axis, dim):
+    ways, here, step = (lax.axis_size(axis), lax.axis_index(axis), shard.shape[dim])
+    shape = [n * ways if d == dim else n for d, n in enumerate(shard.shape)]
+    full = lax.dynamic_update_slice_in_dim(
+        jnp.zeros(shape, shard.dtype), shard, here * step, axis=dim
+    )
+    going_up = going_down = shard
+    for far in range(1, ways // 2 + 1):
+        going_up = lax.ppermute(going_up, axis, [(d, (d + 1) % ways) for d in range(ways)])
+        full = lax.dynamic_update_slice_in_dim(full, going_up, (here - far) % ways * step, axis=dim)
+        if 2 * far < ways:
+            going_down = lax.ppermute(going_down, axis, [(d, (d - 1) % ways) for d in range(ways)])
+            full = lax.dynamic_update_slice_in_dim(
+                full, going_down, (here + far) % ways * step, axis=dim
+            )
+    return full
 
 
 def contrast_table(defocus, width):
@@ -67,7 +85,7 @@
     slice_start = lax.axis_index("img") * slice_width
     limit_float = term_limit.astype(jnp.float32)
     moved_images = lax.all_to_all(back_images, "img", split_axis=1, concat_axis=0, tiled=True)
-    every_post = lax.all_gather(posterior, "img", axis=1, tiled=True)
+    every_post = ring_gather(posterior, "img", 1)
     focus_all, limit_all = (
         lax.all_gather(defocus, "img", axis=0, tiled=True),
         lax.all_gather(limit_float, "img", axis=0, tiled=True),

time: 115 us -> 124 us (1.078)
  blocking collectives: 61.5 us -> 65.6 us
  waiting for transfers between devices: 0.01 us -> 3.46 us
  starting transfers between devices: 4.26 us -> 5.65 us
    all_gather x1, blocking collectives: 5.05 us -> 15.3 us  [shards(): lax.all_gather(defocus, 'img', axis=0, tiled=True)]
    all_gather x1 -> x0, blocking collectives: 6.34 us -> none  [shards(): every_post = lax.all_gather(posterior, 'img', axis=1, tiled=True)]
    ppermute x0 -> x3, waiting for transfers between devices: none -> 3.46 us  [the longest x2 3.46 us: ring_gather(): lax.ppermute(going_up, axis, [(d, (d + 1) % ways) for d in range(ways)])]
    ppermute x0 -> x3, starting transfers between devices: none -> 2.13 us  [the longest x1 1.73 us: ring_gather(): lax.ppermute(going_down, axis, [(d, (d - 1) % ways) for d in range(ways)])]
  transfers between devices with their start and end apart: 1 -> 4, of which waited for: 0 -> 1; matrix products, arithmetic and copies ran while one was open for 28% -> 17% of each run, Pallas kernels for 0% -> 0%
where the time goes in v1:
time: 124 us
  blocking collectives  65.6 us (53%)
  matrix products  31 us (25%)
  other arithmetic  12.3 us (10%)
  starting transfers between devices  5.65 us (5%)
  local copies, waits for them, and re-layouts  5.14 us (4%)
  waiting for transfers between devices  3.46 us (3%)
    pmax x1, blocking collectives, shards(): row_peak = lax.pmax(local_peak, 'proj')  23.1 us
    psum x1, blocking collectives, shards(): row_mass = lax.psum(local_mass, 'proj')  17.1 us
    all_gather x1, blocking collectives, shards(): lax.all_gather(defocus, 'img', axis=0, tiled=True)  15.3 us
    dot_general x1, matrix products, shards(): lax.dot_general(projections, weighted, contract, preferred_element_type=j...  12.5 us
    dot_general x1, matrix products, slice_weight_sums(): jnp.einsum('jbi,bif->bjf', every_post, rebuilt, preferred_element_type=jn...  9.4 us
    convert_element_type x1, other arithmetic, image_terms(): back_images = (keep_mask * contrast * values).astype(jnp.bfloat16)  8.43 us
    dot_general x1, matrix products, shards(): lax.dot_general(proj_sq, weighted_sq, contract, preferred_element_type=jn...  8.17 us
    all_gather x1, blocking collectives, shards(): every_evidence = lax.all_gather(log_evidence, 'img', axis=0, tiled=True)  5.05 us
  transfers between devices with their start and end apart: 4, of which 1 were waited for; matrix products, arithmetic and copies ran while one was open for 17% of the time, Pallas kernels for 0%

profile of v1, /device:TPU:0, one launch (start us, length us, event | category | flops | bytes accessed | tf_op | source)
XLA Modules:
  0.0 124.1 jit_solution(16071978938008712671)
XLA Ops:
  0.6 0.0 copy-start.3
  0.6 0.0 copy-start.5
  0.7 0.7 broadcast_multiply_fusion.1
  1.3 1.6 %copy.13 = bf16[128,4096]{0,1:T(8,128)(2,1)S(1)} copy(bf16[128,4096]{1,0:T(8,128)(2,1)} %param.7) | data formatting | bytes 2097152 | tf_op args[0]
  3.0 0.0 copy-done.3
  3.0 0.0 copy-done.5
  3.0 0.0 copy-start.1
  3.0 0.0 copy-start.4
  3.0 12.5 %convolution_bitcast_fusion = f32[320,128]{1,0:T(8,128)S(1)} fusion(bf16[320,4096]{1,0:T(8,128)(2,1)} %param.8, bf16[128,4096]{0,1:T(8,128)(2,1)S(1)} %copy.13, f32[4096]{0:T(1024)S(1)} %add_multiply_fusion, f32[128]{0:T(128)S(1)} %broadcast_multiply_fusion.1, f32[4096]{0:T(1024)S(1)} %copy-done.5, s32[128]{0:T(128)S(1)} %copy-done.3), kind=kOutput, calls=%fused_computation.19 | convolution fusion | flops 339738624 | bytes 3867648 | tf_op jit(solution)/shard_map/dot_general | solution.py:68
  15.5 0.0 copy-done.1
  15.5 0.0 copy-done.4
  15.5 8.2 %fusion.32 = (f32[128]{0:T(128)S(1)}, f32[320,128]{1,0:T(8,128)S(1)}) fusion(s32[128]{0:T(128)S(1)} %copy-done.1, s32[320]{0:T(512)S(1)} %iota_add_fusion, f32[320,128]{1,0:T(8,128)S(1)} %convolution_bitcast_fusion, f32[4096]{0:T(1024)S(1)} %add_multiply_fusion, f32[128]{0:T(128)S(1)} %broadcast_multiply_fusion.1, f32[4096]{0:T(1024)S(1)} %copy-done.5, ...), kind=kOutput, calls=%fused_computation.47 | convolution fusion | flops 343351168 | bytes 2985216 | tf_op jit(solution)/shard_map/dot_general | solution.py:69
  23.7 23.1 %pmax.7 = f32[128]{0:T(128)S(1)} all-reduce(f32[128]{0:T(128)S(1)} %get-tuple-element.4), channel_id=1, replica_groups=mesh['img'=4,'proj'=8] {'proj'}, use_global_device_ids=true, to_apply=%region_1.2 | all-reduce | flops 128 | bytes 1024 | tf_op jit(solution)/shard_map/pmax | solution.py:75
  46.8 0.1 fusion.35
  46.9 17.1 %psum.7 = f32[128]{0:T(128)S(1)} all-reduce(f32[128]{0:T(128)S(1)} %fusion.35), channel_id=1, replica_groups=mesh['img'=4,'proj'=8] {'proj'}, use_global_device_ids=true, to_apply=%region_3.4 | all-reduce | flops 128 | bytes 1024 | tf_op jit(solution)/shard_map/psum | solution.py:78
  64.1 0.1 constant_dynamic-update-slice_fusion.3
  64.2 0.1 collective-permute-start
  64.3 1.7 %collective-permute-start.1 = (bf16[320,128]{1,0:T(8,128)(2,1)S(1)}, bf16[320,128]{1,0:T(8,128)(2,1)S(1)}, u32[]{:S(2)}, u32[]{:S(2)}) collective-permute-start(bf16[320,128]{1,0:T(8,128)(2,1)S(1)} %get-tuple-element.3), channel_id=1, source_target_pairs={{0,24},{8,0},{16,8},{24,16},{1,25},{9,1},{17,9},{25,17},{2,26},{10... | collective-permute-start | bytes 245768 | tf_op jit(solution)/shard_map/ppermute | solution.py:22
  66.0 8.4 %fusion.2 = bf16[128,4096]{0,1:T(8,128)(2,1)S(1)} fusion(bf16[128,4096]{0,1:T(8,128)(2,1)S(1)} %copy.13, f32[4096]{0:T(1024)S(1)} %add_multiply_fusion, f32[128]{0:T(128)S(1)} %broadcast_multiply_fusion.1, s32[128]{0:T(128)S(1)} %copy-done.3), kind=kLoop, calls=%fused_computation.8 | loop fusion | flops 3670016 | bytes 2114560 | tf_op jit(solution)/shard_map/convert_element_type | solution.py:41
  74.5 0.0 copy-start.2
  74.5 0.0 copy-start.6
  74.5 1.3 %copy.14 = bf16[128,4,1024]{2,0,1:T(8,128)(2,1)} copy(bf16[128,4,1024]{0,2,1:T(8,128)(2,1)S(1)} %bitcast.26) | data formatting | bytes 2097152 | tf_op jit(solution)/shard_map/all_to_all | solution.py:87
  75.8 3.5 %all-to-all-start = ((bf16[128,4,1024]{2,0,1:T(8,128)(2,1)}), bf16[128,4,1024]{2,0,1:T(8,128)(2,1)S(1)}, u32[]{:S(2)}, u32[]{:S(2)}) async-start(bf16[128,4,1024]{2,0,1:T(8,128)(2,1)} %copy.14), calls=%async_computation | async-start | bytes 2097152 | tf_op jit(solution)/shard_map/all_to_all | solution.py:87
  79.3 0.0 copy-done.2
  79.4 15.3 %all-gather.1 = f32[4,1,128]{2,1,0:T(1,128)S(1)} all-gather(f32[1,1,128]{2,1,0:T(1,128)S(1)} %bitcast.30), channel_id=1, replica_groups=mesh['img'=4,'proj'=8] {'img'}, dimensions={0}, use_global_device_ids=true | all-gather | bytes 2560 | tf_op jit(solution)/shard_map/all_gather | solution.py:90
  94.6 5.0 %all-gather.2 = f32[4,1,128]{2,1,0:T(1,128)S(1)} all-gather(f32[1,1,128]{2,1,0:T(1,128)S(1)} %bitcast.29), channel_id=1, replica_groups=mesh['img'=4,'proj'=8] {'img'}, dimensions={0}, use_global_device_ids=true | all-gather | bytes 2560 | tf_op jit(solution)/shard_map/all_gather | solution.py:104
  99.7 0.5 broadcast.87
  100.2 0.7 reduce.3
  100.9 0.1 reshape.73
  100.9 0.0 copy-done.6
  100.9 0.2 fusion.37
  101.1 0.6 reshape.74
  101.7 5.0 %all-gather = f32[4,1,128]{2,1,0:T(1,128)S(1)} all-gather(f32[1,1,128]{2,1,0:T(1,128)S(1)} %convert_bitcast_fusion), channel_id=1, replica_groups=mesh['img'=4,'proj'=8] {'img'}, dimensions={0}, use_global_device_ids=true | all-gather | bytes 2560 | tf_op jit(solution)/shard_map/all_gather | solution.py:91
  106.8 0.0 collective-permute-done
  106.8 0.3 collective-permute-start.2
  107.2 0.0 collective-permute-done.1
  107.2 3.5 %collective-permute-done.2 = bf16[320,128]{1,0:T(8,128)(2,1)S(1)} collective-permute-done((bf16[320,128]{1,0:T(8,128)(2,1)S(1)}, bf16[320,128]{1,0:T(8,128)(2,1)S(1)}, u32[]{:S(2)}, u32[]{:S(2)}) %collective-permute-start.2) | collective-permute-done | bytes 81952 | tf_op jit(solution)/shard_map/ppermute | solution.py:19
  110.7 9.4 %convolution_convert_fusion = bf16[4,320,1024]{2,1,0:T(8,128)(2,1)} fusion(f32[1024]{0:T(1024)S(1)} %add_multiply_fusion.1, f32[4,128]{1,0:T(4,128)S(1)} %bitcast.28, f32[4,128]{1,0:T(4,128)S(1)} %bitcast.27, f32[1024]{0:T(1024)S(1)} %add_convert_fusion, bf16[320,512]{1,0:T(8,128)(2,1)S(1)} %constant_dynamic-update-slice_fusion), kind=kOutput, calls=%fused_computation.14 | convolution fusion | flops 340000768 | bytes 2961408 | tf_op jit(solution)/shard_map/jbi,bif->bjf/dot_general | solution.py:53
  120.1 0.0 all-to-all-done
  120.1 0.0 copy-start
  120.1 0.8 convolution_convert_fusion.1
  120.9 0.9 copy-done
  121.8 1.2 convert_reduce_fusion
  123.1 1.1 divide_convert_fusion
  (12 shorter events, 0.1 us)
Async XLA Ops:
  0.6 2.3 %copy-start.3 = (s32[128]{0:T(128)S(1)}, s32[128]{0:T(128)}, u32[]{:S(2)}) copy-start(s32[128]{0:T(128)} %param.12) | copy-start | bytes 1540
  0.6 2.3 %copy-start.5 = (f32[4096]{0:T(1024)S(1)}, f32[4096]{0:T(1024)}, u32[]{:S(2)}) copy-start(f32[4096]{0:T(1024)} %param.9) | copy-start | bytes 49156
  3.0 12.5 %copy-start.1 = (s32[128]{0:T(128)S(1)}, s32[128]{0:T(128)}, u32[]{:S(2)}) copy-start(s32[128]{0:T(128)} %param.11) | copy-start | bytes 1540
  3.0 12.5 %copy-start.4 = (bf16[320,4096]{1,0:T(8,128)(2,1)S(1)}, bf16[320,4096]{1,0:T(8,128)(2,1)}, u32[]{:S(2)}) copy-start(bf16[320,4096]{1,0:T(8,128)(2,1)} %param.8) | copy-start | bytes 7864324
  64.2 42.6 %collective-permute-start = (bf16[320,128]{1,0:T(8,128)(2,1)S(1)}, bf16[320,128]{1,0:T(8,128)(2,1)S(1)}, u32[]{:S(2)}, u32[]{:S(2)}) collective-permute-start(bf16[320,128]{1,0:T(8,128)(2,1)S(1)} %get-tuple-element.3), channel_id=1, source_target_pairs={{0,8},{8,16},{16,24},{24,0},{1,9},{9,17},{17,25},{25,1},{2,10},{10... | collective-permute-start | bytes 245768 | tf_op jit(solution)/shard_map/ppermute | solution.py:19
  64.3 42.9 %collective-permute-start.1 = (bf16[320,128]{1,0:T(8,128)(2,1)S(1)}, bf16[320,128]{1,0:T(8,128)(2,1)S(1)}, u32[]{:S(2)}, u32[]{:S(2)}) collective-permute-start(bf16[320,128]{1,0:T(8,128)(2,1)S(1)} %get-tuple-element.3), channel_id=1, source_target_pairs={{0,24},{8,0},{16,8},{24,16},{1,25},{9,1},{17,9},{25,17},{2,26},{10... | collective-permute-start | bytes 245768 | tf_op jit(solution)/shard_map/ppermute | solution.py:22
  74.5 4.9 %copy-start.2 = (f32[128]{0:T(128)S(1)}, f32[128]{0:T(128)}, u32[]{:S(2)}) copy-start(f32[128]{0:T(128)} %param.10) | copy-start | bytes 1540
  74.5 26.5 %copy-start.6 = (s32[16]{0:T(128)S(1)}, s32[16]{0:T(128)}, u32[]{:S(2)}) copy-start(s32[16]{0:T(128)} %param.13) | copy-start | bytes 196
  75.8 44.3 %all-to-all-start = ((bf16[128,4,1024]{2,0,1:T(8,128)(2,1)}), bf16[128,4,1024]{2,0,1:T(8,128)(2,1)S(1)}, u32[]{:S(2)}, u32[]{:S(2)}) async-start(bf16[128,4,1024]{2,0,1:T(8,128)(2,1)} %copy.14), calls=%async_computation | async-start | bytes 2097152 | tf_op jit(solution)/shard_map/all_to_all | solution.py:87
  106.8 3.9 %collective-permute-start.2 = (bf16[320,128]{1,0:T(8,128)(2,1)S(1)}, bf16[320,128]{1,0:T(8,128)(2,1)S(1)}, u32[]{:S(2)}, u32[]{:S(2)}) collective-permute-start(bf16[320,128]{1,0:T(8,128)(2,1)S(1)} %collective-permute-done), channel_id=1, source_target_pairs={{0,8},{8,16},{16,24},{24,0},{1,9},{9,17},{17,25},{25,1},{2,10},{10... | collective-permute-start | bytes 245768 | tf_op jit(solution)/shard_map/ppermute | solution.py:19
  120.1 1.7 %copy-start = (bf16[4,320,1024]{2,1,0:T(8,128)(2,1)S(1)}, bf16[4,320,1024]{2,1,0:T(8,128)(2,1)}, u32[]{:S(2)}) copy-start(bf16[4,320,1024]{2,1,0:T(8,128)(2,1)} %convolution_convert_fusion) | copy-start | bytes 7864324
